TPU v7x, 512 devices: a whole 4x4x16 slice. The times are simulated.
512 devices in a mesh: contract: 32 (over z, y_lo), out: 16 (over y_hi, x, core).
Axes of the slice: x: 4, y: 4 (y_hi: 2, y_lo: 2; y = y_hi * 2 + y_lo), z: 16, core: 2. Of those that a mesh axis runs over, the one named last changes fastest.
Arguments:
- chol: bfloat16 [128, 1024, 640], P('out', 'contract'), may hold values from -1.1953125 to 1.1953125
- amplitudes: bfloat16 [128, 32768], P('out', 'contract'), may hold values from -0.0625 to 0.0625
- tile_pairs: int32 [64, 2], replicated, may hold values from 0 to 7, as said below
- partner: int32 [64], replicated, may hold values from 0 to 63, as said below
- pair_swap: int32 [128], replicated, may hold values from 0 to 127, as said below
Outputs:
- residual: float32 [64, 128, 256], P('out', 'contract')
Inputs may be any that keep to these rules, and one draw needn't show every extreme that they name: `tile_pairs`: each ordered pair of tiles of 0 to 7 stands at exactly one slot. partner[s] is the slot holding the pair of slot s reversed; a diagonal pair is its own partner. `pair_swap`: an involution without fixed points that maps each aligned block of 4 pairs into itself.
All inputs are finite; a program needn't handle non-finite values.
Results may differ from a plain program's by a relative error of at most 0.0029.
Values may be sent and summed in bfloat16 or wider, within the bound.
No kernel may reach another device: no remote copies, remote signals or barrier semaphores. Data moves between devices by JAX's collectives and lax.ppermute only.
A program may use at most 128 MiB of HBM per device.

v0:
```python
import jax
import jax.numpy as jnp
from jax import lax
from jax.sharding import Mesh
from jax.sharding import PartitionSpec as P

TS = 16
CONTRACT = ("contract_0", "contract_1")


def broadcast_by_axis(array, axes, root):
    array = jnp.where(lax.axis_index(axes) == root, array, jnp.zeros_like(array))
    for axis in axes:
        array = lax.psum(array, axis)
    return array


def cut_along(array, dim, count):
    before, after = (array.shape[:dim], array.shape[dim + 1 :])
    return jnp.moveaxis(array.reshape(*before, count, -1, *after), dim, 0)


def sum_at_owner(array, axis, dim):
    count = lax.axis_size(axis)
    parts = lax.all_to_all(cut_along(array, dim, count), axis, 0, 0, tiled=True)
    return jnp.sum(parts, axis=0)


def laid_out(parts, dim):
    lengths = list(parts.shape[1:])
    lengths[dim] *= parts.shape[0]
    return jnp.moveaxis(parts, 0, dim).reshape(lengths)


def sent_to_all(array, axis):
    count = lax.axis_size(axis)
    return lax.all_to_all(
        jnp.broadcast_to(array[None], (count, *array.shape)), axis, 0, 0, tiled=True
    )


def collect(array, axis, dim):
    return laid_out(sent_to_all(array, axis), dim)


def pick_tile(source, tile):
    return lax.dynamic_slice_in_dim(source, tile * TS, TS, 0)


def on_device(chol, amplitudes, tile_pairs, partner, pair_swap):
    out_count = lax.axis_size("out")
    con_count = lax.axis_size(CONTRACT)
    out_index = lax.axis_index("out")
    con_index = lax.axis_index(CONTRACT)
    local_window = broadcast_by_axis(chol, CONTRACT, 0)
    rows_all, window, amps_all = (
        lax.all_gather(chol, "out", axis=0, tiled=True),
        lax.all_gather(local_window, "out", axis=0, tiled=True),
        lax.all_gather(amplitudes, "out", axis=0, tiled=True),
    )
    slot_count = tile_pairs.shape[0] // out_count
    first = out_index * slot_count
    pairs = lax.dynamic_slice_in_dim(tile_pairs, first, slot_count, 0)
    left = jax.vmap(pick_tile, (None, 0))(rows_all, pairs[:, 0])
    right = jax.vmap(pick_tile, (None, 0))(window, pairs[:, 1])
    integral = jnp.einsum(
        "sacp,sbdp->sabcd", left, right, preferred_element_type=jnp.float32
    ).astype(jnp.bfloat16)
    flat = integral.reshape(slot_count * TS * TS, -1)
    occ_dev = amps_all.shape[0] // con_count
    ladder = sum_at_owner(
        lax.dot_general(
            amps_all, flat, (((1,), (1,)), ((), ())), preferred_element_type=jnp.float32
        ),
        CONTRACT,
        0,
    )
    ladder = jnp.transpose(ladder.reshape(occ_dev, slot_count, TS, TS), (1, 0, 2, 3))
    own_swap = (
        lax.dynamic_slice_in_dim(pair_swap, con_index * occ_dev, occ_dev, 0) - con_index * occ_dev
    )
    turned = jnp.transpose(jnp.take(ladder, own_swap, axis=1), (0, 1, 3, 2))
    turned = turned.reshape(slot_count, occ_dev, TS * TS)
    every = collect(turned, "out", 0)
    wanted = lax.dynamic_slice_in_dim(partner, first, slot_count, 0)
    mirror = jnp.take(every, wanted, axis=0)
    return ladder.reshape(slot_count, occ_dev, TS * TS) + mirror


def solution(mesh):
    torus = Mesh(
        mesh.devices.reshape(16, 2, mesh.shape["out"]), ("contract_0", "contract_1", "out")
    )
    in_specs = (P("out", CONTRACT, None), P("out", CONTRACT), P(), P(), P())
    out_specs = P("out", CONTRACT, None)
    return jax.shard_map(
        on_device, mesh=torus, in_specs=in_specs, out_specs=out_specs, check_vma=False
    )
```

profile of v0, /device:TPU:1, one launch (start us, length us, event | category | flops | bytes accessed | tf_op | source)
XLA Modules:
  0.0 417.8 jit_solution(8291045161352591324)
XLA Ops:
  7.4 0.0 copy-start
  7.4 0.0 all-reduce.5.cloned.1.call-start
  7.4 1.7 broadcast_select_fusion
  9.1 0.0 all-reduce.5.cloned.1.call-update
  9.1 0.0 all-reduce.7.cloned.1.call-start
  9.2 133.9 %all-reduce.5.cloned.1.call-done = bf16[8,32,640]{2,1,0:T(8,128)(2,1)} async-done(((bf16[8,32,640]{2,1,0:T(8,128)(2,1)}), bf16[8,32,640]{2,1,0:T(8,128)(2,1)}) %all-reduce.5.cloned.1.call-update) | async-done | bytes 327696 | tf_op jit(solution)/shard_map/psum | solution.py:14
  143.0 0.0 all-reduce.7.cloned.1.call-update
  143.1 0.0 all-gather.5.cloned.1.call-start
  143.1 0.5 all-gather.5.cloned.1.call-update
  143.6 0.0 all-gather.3.cloned.1.call-start
  143.7 55.1 %all-reduce.7.cloned.1.call-done = bf16[8,32,640]{2,1,0:T(8,128)(2,1)} async-done(((bf16[8,32,640]{2,1,0:T(8,128)(2,1)}), bf16[8,32,640]{2,1,0:T(8,128)(2,1)}) %all-reduce.7.cloned.1.call-update) | async-done | bytes 327696 | tf_op jit(solution)/shard_map/psum | solution.py:14
  198.8 0.0 all-gather.3.cloned.1.call-update
  198.8 0.0 copy-done
  198.8 0.1 constant_dynamic-slice_fusion
  198.9 25.7 %all_gather.11 = bf16[128,1024]{1,0:T(8,128)(2,1)S(1)} all-gather(bf16[8,1024]{1,0:T(8,128)(2,1)} %param.6), channel_id=1, replica_groups=mesh['contract_0'=16,'contract_1'=2,'out'=16] {'out'}, dimensions={0}, use_global_device_ids=true | all-gather | bytes 278528 | tf_op jit(solution)/shard_map/all_gather | solution.py:59
  224.6 4.9 %all-gather.5.cloned.1.call-done = bf16[128,32,640]{2,1,0:T(8,128)(2,1)} async-done(((bf16[8,32,640]{2,1,0:T(8,128)(2,1)}), bf16[128,32,640]{2,1,0:T(8,128)(2,1)}) %all-gather.5.cloned.1.call-update) | async-done | bytes 5242896 | tf_op jit(solution)/shard_map/all_gather | solution.py:57
  229.5 3.5 gather_fusion.1
  233.0 74.3 %all-gather.3.cloned.1.call-done = bf16[128,32,640]{2,1,0:T(8,128)(2,1)} async-done(((bf16[8,32,640]{2,1,0:T(8,128)(2,1)}), bf16[128,32,640]{2,1,0:T(8,128)(2,1)}) %all-gather.3.cloned.1.call-update) | async-done | bytes 5242896 | tf_op jit(solution)/shard_map/all_gather | solution.py:58
  307.3 4.9 %gather_fusion = bf16[4,16,32,640]{3,2,1,0:T(8,128)(2,1)} fusion(bf16[128,32,640]{2,1,0:T(8,128)(2,1)} %all-gather.3.cloned.1.call-done, s32[4]{0:T(128)S(1)} %get-tuple-element.9), kind=kCustom, calls=%fused_computation | custom fusion | bytes 5242928 | tf_op jit(solution)/shard_map/vmap()/gather | solution.py:47
  312.3 10.4 %convert_bitcast_fusion = bf16[4,16,16,32,32]{3,4,1,2,0:T(8,128)(2,1)} fusion(bf16[4,16,32,640]{3,2,1,0:T(8,128)(2,1)S(1)} %gather_fusion.1, bf16[4,16,32,640]{3,2,1,0:T(8,128)(2,1)} %gather_fusion), kind=kOutput, calls=%fused_computation.4 | convolution fusion | flops 1343225856 | bytes 7340032 | tf_op jit(solution)/shard_map/sacp,sbdp->sabcd/dot_general | solution.py:66
  322.6 11.5 %copy.9 = bf16[4,16,16,32,32]{4,3,2,1,0:T(8,128)(2,1)} copy(bf16[4,16,16,32,32]{3,4,1,2,0:T(8,128)(2,1)} %convert_bitcast_fusion) | data formatting | bytes 4194304 | tf_op jit(solution)/shard_map/convert_element_type | solution.py:68
  334.1 11.3 %reshape.26 = bf16[1024,1024]{1,0:T(8,128)(2,1)S(1)} reshape(bf16[4,16,16,32,32]{4,3,2,1,0:T(8,128)(2,1)} %copy.9) | data formatting | bytes 4194304 | tf_op jit(solution)/shard_map/reshape | solution.py:69
  345.4 0.0 copy-start.1
  345.4 0.8 convolution_bitcast_fusion
  346.3 0.0 copy-start.2
  346.3 0.9 reshape.27
  347.2 12.3 %all-to-all-start = ((f32[32,4,1024]{2,1,0:T(4,128)}), f32[32,4,1024]{2,1,0:T(4,128)S(1)}, u32[]{:S(2)}, u32[]{:S(2)}) async-start(f32[32,4,1024]{2,1,0:T(4,128)} %reshape.27), calls=%async_computation | async-start | bytes 1048576 | tf_op jit(solution)/shard_map/all_to_all | solution.py:25
  359.6 0.0 copy-done.1
  359.6 0.1 compare_and_fusion
  359.7 32.0 %all-to-all-done = f32[32,4,1024]{2,1,0:T(4,128)S(1)} async-done(((f32[32,4,1024]{2,1,0:T(4,128)}), f32[32,4,1024]{2,1,0:T(4,128)S(1)}, u32[]{:S(2)}, u32[]{:S(2)}) %all-to-all-start) | async-done | bytes 524320 | tf_op jit(solution)/shard_map/all_to_all | solution.py:25
  391.7 0.1 reduce_sum.9
  391.8 0.1 reshape.28
  391.9 0.6 gather_fusion.2
  392.5 0.1 select_bitcast_fusion
  392.6 0.1 copy.11
  392.7 0.1 broadcast_in_dim.41
  392.8 0.8 broadcast_in_dim.42
  393.5 6.8 %all-to-all-start.1 = ((f32[16,4,4,256]{3,2,1,0:T(4,128)}), f32[16,4,4,256]{3,2,1,0:T(4,128)S(1)}, u32[]{:S(2)}, u32[]{:S(2)}) async-start(f32[16,4,4,256]{3,2,1,0:T(4,128)} %broadcast_in_dim.42), calls=%async_computation.1 | async-start | bytes 524288 | tf_op jit(solution)/shard_map/all_to_all | solution.py:37
  400.4 0.0 copy-done.2
  400.4 0.1 compare_and_fusion.1
  400.5 0.1 reshape.63
  400.6 8.5 %all-to-all-done.1 = f32[16,4,4,256]{3,2,1,0:T(4,128)S(1)} async-done(((f32[16,4,4,256]{3,2,1,0:T(4,128)}), f32[16,4,4,256]{3,2,1,0:T(4,128)S(1)}, u32[]{:S(2)}, u32[]{:S(2)}) %all-to-all-start.1) | async-done | bytes 262176 | tf_op jit(solution)/shard_map/all_to_all | solution.py:37
  409.1 0.6 gather_fusion.3
  409.6 0.7 copy_add_fusion
  (3 shorter events, 0.0 us)
Async XLA Ops:
  7.4 191.4 %copy-start = (s32[64,2]{0,1:T(2,128)S(1)}, s32[64,2]{0,1:T(2,128)}, u32[]{:S(2)}) copy-start(s32[64,2]{0,1:T(2,128)} %param.7) | copy-start | bytes 1540
  7.4 135.7 %all-reduce.5.cloned.1.call-start = ((), (), s32[]{:S(2)}) async-start(), calls=%async_computation.2 | async-start | bytes 655360 | tf_op jit(solution)/shard_map/psum | solution.py:14
  9.1 189.6 %all-reduce.7.cloned.1.call-start = ((), (), s32[]{:S(2)}) async-start(), calls=%async_computation.3 | async-start | bytes 655360 | tf_op jit(solution)/shard_map/psum | solution.py:14
  143.1 86.4 %all-gather.5.cloned.1.call-start = ((), (), s32[]{:S(2)}) async-start(), calls=%async_computation.5 | async-start | bytes 5570560 | tf_op jit(solution)/shard_map/all_gather | solution.py:57
  143.6 163.7 %all-gather.3.cloned.1.call-start = ((), (), s32[]{:S(2)}) async-start(), calls=%async_computation.4 | async-start | bytes 5570560 | tf_op jit(solution)/shard_map/all_gather | solution.py:58
  345.4 14.1 %copy-start.1 = (s32[128]{0:T(128)S(1)}, s32[128]{0:T(128)}, u32[]{:S(2)}) copy-start(s32[128]{0:T(128)} %param.9) | copy-start | bytes 1540
  346.3 54.1 %copy-start.2 = (s32[64]{0:T(128)S(1)}, s32[64]{0:T(128)}, u32[]{:S(2)}) copy-start(s32[64]{0:T(128)} %param.8) | copy-start | bytes 772
  347.2 44.5 %all-to-all-start = ((f32[32,4,1024]{2,1,0:T(4,128)}), f32[32,4,1024]{2,1,0:T(4,128)S(1)}, u32[]{:S(2)}, u32[]{:S(2)}) async-start(f32[32,4,1024]{2,1,0:T(4,128)} %reshape.27), calls=%async_computation | async-start | bytes 1048576 | tf_op jit(solution)/shard_map/all_to_all | solution.py:25
  393.5 15.5 %all-to-all-start.1 = ((f32[16,4,4,256]{3,2,1,0:T(4,128)}), f32[16,4,4,256]{3,2,1,0:T(4,128)S(1)}, u32[]{:S(2)}, u32[]{:S(2)}) async-start(f32[16,4,4,256]{3,2,1,0:T(4,128)} %broadcast_in_dim.42), calls=%async_computation.1 | async-start | bytes 524288 | tf_op jit(solution)/shard_map/all_to_all | solution.py:37
Sparse Core Ops, SparseCore 0:
  10.5 132.4 all-reduce.4
  145.9 52.8 all-reduce.6
Sparse Core Ops, SparseCore 1:
  146.8 82.6 all-gather.4
  232.7 74.6 all-gather.2
where the time goes:
time: 419 us; the launch traced here: 418 us
  waiting for transfers between devices  309 us (74%)
  local copies, waits for them, and re-layouts  34.5 us (8%)
  blocking collectives  25.7 us (6%)
  starting transfers between devices  19.3 us (5%)
  between operations  15 us (4%)
  matrix products  11.2 us (3%)
    psum x2, waiting for transfers between devices, broadcast_by_axis(): array = lax.psum(array, axis)  189 us
    all_gather x1, waiting for transfers between devices, on_device(): lax.all_gather(local_window, 'out', axis=0, tiled=True)  74.3 us
    all_to_all x1, waiting for transfers between devices, sum_at_owner(): parts = lax.all_to_all(cut_along(array, dim, count), axis, 0, 0, tiled=True)  32 us
    all_gather x1, blocking collectives, on_device(): lax.all_gather(amplitudes, 'out', axis=0, tiled=True)  25.7 us
    all_to_all x1, starting transfers between devices, sum_at_owner(): parts = lax.all_to_all(cut_along(array, dim, count), axis, 0, 0, tiled=True)  12.3 us
    convert_element_type x1, local copies, waits for them, and re-layouts, on_device(): integral = jnp.einsum('sacp,sbdp->sabcd', left, right, preferred_element_...  11.5 us
    reshape x1, local copies, waits for them, and re-layouts, on_device(): flat = integral.reshape(slot_count * TS * TS, -1)  11.3 us
    dot_general x1, matrix products, on_device(): jnp.einsum('sacp,sbdp->sabcd', left, right, preferred_element_type=jnp.fl...  10.4 us
  transfers between devices with their start and end apart: 6, of which 6 were waited for; matrix products, arithmetic and copies ran while one was open for 1% of the time, Pallas kernels for 0%

commit v1 on v0

--- a/solution.py
+++ b/solution.py
@@ -11,7 +11,7 @@
 def broadcast_by_axis(array, axes, root):
     array = jnp.where(lax.axis_index(axes) == root, array, jnp.zeros_like(array))
     for axis in axes:
-        array = lax.psum(array, axis)
+        array = jnp.sum(lax.all_gather(array, axis), axis=0)
     return array
 
 

time: 419 us -> 358 us (0.85)
  waiting for transfers between devices: 309 us -> 231 us
  blocking collectives: 25.7 us -> 41 us
  other arithmetic: 2.78 us -> 7.01 us
    psum x2 -> x0, waiting for transfers between devices: 189 us -> none  [broadcast_by_axis(): array = lax.psum(array, axis)]
    all_gather x0 -> x1, waiting for transfers between devices: none -> 78.7 us  [broadcast_by_axis(): array = jnp.sum(lax.all_gather(array, axis), axis=0)]
    all_gather x1, waiting for transfers between devices: 4.89 us -> 37.2 us  [on_device(): lax.all_gather(chol, 'out', axis=0, tiled=True)]
    all_gather x1, blocking collectives: 25.7 us -> 34.4 us  [on_device(): lax.all_gather(amplitudes, 'out', axis=0, tiled=True)]
    all_gather x0 -> x1, blocking collectives: none -> 6.59 us  [broadcast_by_axis(): array = jnp.sum(lax.all_gather(array, axis), axis=0)]
    reduce_sum x0 -> x2, other arithmetic: none -> 4.2 us  [broadcast_by_axis(): array = jnp.sum(lax.all_gather(array, axis), axis=0)]
  transfers between devices with their start and end apart: 6 -> 5, of which waited for: 6 -> 5; matrix products, arithmetic and copies ran while one was open for 1% -> 2% of each run, Pallas kernels for 0% -> 0%
where the time goes in v1:
time: 358 us; the launch traced here: 357 us
  waiting for transfers between devices  231 us (65%)
  blocking collectives  41 us (11%)
  local copies, waits for them, and re-layouts  34.5 us (10%)
  starting transfers between devices  19.2 us (5%)
  between operations  13.2 us (4%)
  matrix products  11.2 us (3%)
  other arithmetic  7.01 us (2%)
    all_gather x1, waiting for transfers between devices, broadcast_by_axis(): array = jnp.sum(lax.all_gather(array, axis), axis=0)  78.7 us
    all_gather x1, waiting for transfers between devices, on_device(): lax.all_gather(local_window, 'out', axis=0, tiled=True)  74 us
    all_gather x1, waiting for transfers between devices, on_device(): lax.all_gather(chol, 'out', axis=0, tiled=True)  37.2 us
    all_gather x1, blocking collectives, on_device(): lax.all_gather(amplitudes, 'out', axis=0, tiled=True)  34.4 us
    all_to_all x1, waiting for transfers between devices, sum_at_owner(): parts = lax.all_to_all(cut_along(array, dim, count), axis, 0, 0, tiled=True)  32 us
    all_to_all x1, starting transfers between devices, sum_at_owner(): parts = lax.all_to_all(cut_along(array, dim, count), axis, 0, 0, tiled=True)  12.3 us
    convert_element_type x1, local copies, waits for them, and re-layouts, on_device(): integral = jnp.einsum('sacp,sbdp->sabcd', left, right, preferred_element_...  11.4 us
    reshape x1, local copies, waits for them, and re-layouts, on_device(): flat = integral.reshape(slot_count * TS * TS, -1)  11.3 us
  transfers between devices with their start and end apart: 5, of which 5 were waited for; matrix products, arithmetic and copies ran while one was open for 2% of the time, Pallas kernels for 0%

profile of v1, /device:TPU:1, one launch (start us, length us, event | category | flops | bytes accessed | tf_op | source)
XLA Modules:
  0.0 357.3 jit_solution(112418371662182392)
XLA Ops:
  6.5 0.0 copy-start
  6.5 0.0 all-gather.10.cloned.1.call-start
  6.5 1.8 broadcast_select_fusion
  8.3 0.0 all-gather.10.cloned.1.call-update
  8.3 0.0 all-gather.8.cloned.1.call-start
  8.4 0.7 all-gather.8.cloned.1.call-update
  9.1 0.0 all-gather.6.cloned.1.call-start
  9.1 78.7 %all-gather.10.cloned.1.call-done = bf16[128,32,640]{2,1,0:T(8,128)(2,1)} async-done(((bf16[8,32,640]{2,1,0:T(8,128)(2,1)}), bf16[128,32,640]{2,1,0:T(8,128)(2,1)}) %all-gather.10.cloned.1.call-update) | async-done | bytes 5242896 | tf_op jit(solution)/shard_map/all_gather | solution.py:14
  87.8 0.0 copy-start.1
  87.8 3.3 reduce_sum.33
  91.1 6.6 %all-gather.1 = bf16[16,32,640]{2,1,0:T(8,128)(2,1)S(1)} all-gather(bf16[8,32,640]{2,1,0:T(8,128)(2,1)S(1)} %reduce_sum.33), channel_id=3, replica_groups=mesh['contract_0'=16,'contract_1'=2,'out'=16] {'contract_1'}, dimensions={0}, use_global_device_ids=true | all-gather | bytes 983040 | tf_op jit(solution)/shard_map/all_gather | solution.py:14
  97.7 0.9 reduce_sum.34
  98.6 0.0 all-gather.6.cloned.1.call-update
  98.6 0.0 copy-done
  98.6 0.1 constant_dynamic-slice_fusion
  98.7 0.0 copy-done.1
  98.7 34.4 %all_gather.27 = bf16[128,1024]{1,0:T(8,128)(2,1)S(1)} all-gather(bf16[8,1024]{1,0:T(8,128)(2,1)S(1)} %copy-done.1), channel_id=1, replica_groups=mesh['contract_0'=16,'contract_1'=2,'out'=16] {'out'}, dimensions={0}, use_global_device_ids=true | all-gather | bytes 278528 | tf_op jit(solution)/shard_map/all_gather | solution.py:59
  133.2 37.2 %all-gather.8.cloned.1.call-done = bf16[128,32,640]{2,1,0:T(8,128)(2,1)} async-done(((bf16[8,32,640]{2,1,0:T(8,128)(2,1)}), bf16[128,32,640]{2,1,0:T(8,128)(2,1)}) %all-gather.8.cloned.1.call-update) | async-done | bytes 5242896 | tf_op jit(solution)/shard_map/all_gather | solution.py:57
  170.3 3.5 gather_fusion.1
  173.8 74.0 %all-gather.6.cloned.1.call-done = bf16[128,32,640]{2,1,0:T(8,128)(2,1)} async-done(((bf16[8,32,640]{2,1,0:T(8,128)(2,1)}), bf16[128,32,640]{2,1,0:T(8,128)(2,1)}) %all-gather.6.cloned.1.call-update) | async-done | bytes 5242896 | tf_op jit(solution)/shard_map/all_gather | solution.py:58
  247.8 4.9 %gather_fusion = bf16[4,16,32,640]{3,2,1,0:T(8,128)(2,1)} fusion(bf16[128,32,640]{2,1,0:T(8,128)(2,1)} %all-gather.6.cloned.1.call-done, s32[4]{0:T(128)S(1)} %get-tuple-element.9), kind=kCustom, calls=%fused_computation | custom fusion | bytes 5242928 | tf_op jit(solution)/shard_map/vmap()/gather | solution.py:47
  252.7 10.3 %convert_bitcast_fusion = bf16[4,16,16,32,32]{3,4,1,2,0:T(8,128)(2,1)} fusion(bf16[4,16,32,640]{3,2,1,0:T(8,128)(2,1)S(1)} %gather_fusion.1, bf16[4,16,32,640]{3,2,1,0:T(8,128)(2,1)} %gather_fusion), kind=kOutput, calls=%fused_computation.4 | convolution fusion | flops 1343225856 | bytes 7340032 | tf_op jit(solution)/shard_map/sacp,sbdp->sabcd/dot_general | solution.py:66
  263.0 11.4 %copy.9 = bf16[4,16,16,32,32]{4,3,2,1,0:T(8,128)(2,1)} copy(bf16[4,16,16,32,32]{3,4,1,2,0:T(8,128)(2,1)} %convert_bitcast_fusion) | data formatting | bytes 4194304 | tf_op jit(solution)/shard_map/convert_element_type | solution.py:68
  274.5 11.3 %reshape.26 = bf16[1024,1024]{1,0:T(8,128)(2,1)S(1)} reshape(bf16[4,16,16,32,32]{4,3,2,1,0:T(8,128)(2,1)} %copy.9) | data formatting | bytes 4194304 | tf_op jit(solution)/shard_map/reshape | solution.py:69
  285.8 0.0 copy-start.2
  285.8 0.8 convolution_bitcast_fusion
  286.7 0.0 copy-start.3
  286.7 0.9 reshape.27
  287.6 12.3 %all-to-all-start = ((f32[32,4,1024]{2,1,0:T(4,128)}), f32[32,4,1024]{2,1,0:T(4,128)S(1)}, u32[]{:S(2)}, u32[]{:S(2)}) async-start(f32[32,4,1024]{2,1,0:T(4,128)} %reshape.27), calls=%async_computation | async-start | bytes 1048576 | tf_op jit(solution)/shard_map/all_to_all | solution.py:25
  299.9 0.0 copy-done.2
  300.0 0.1 compare_and_fusion
  300.0 32.0 %all-to-all-done = f32[32,4,1024]{2,1,0:T(4,128)S(1)} async-done(((f32[32,4,1024]{2,1,0:T(4,128)}), f32[32,4,1024]{2,1,0:T(4,128)S(1)}, u32[]{:S(2)}, u32[]{:S(2)}) %all-to-all-start) | async-done | bytes 524320 | tf_op jit(solution)/shard_map/all_to_all | solution.py:25
  332.1 0.1 reduce_sum.35
  332.2 0.1 reshape.28
  332.3 0.6 gather_fusion.2
  332.9 0.1 select_bitcast_fusion
  332.9 0.1 copy.11
  333.1 0.1 broadcast_in_dim.41
  333.2 0.8 broadcast_in_dim.42
  333.9 6.8 %all-to-all-start.1 = ((f32[16,4,4,256]{3,2,1,0:T(4,128)}), f32[16,4,4,256]{3,2,1,0:T(4,128)S(1)}, u32[]{:S(2)}, u32[]{:S(2)}) async-start(f32[16,4,4,256]{3,2,1,0:T(4,128)} %broadcast_in_dim.42), calls=%async_computation.1 | async-start | bytes 524288 | tf_op jit(solution)/shard_map/all_to_all | solution.py:37
  340.8 0.0 copy-done.3
  340.8 0.1 compare_and_fusion.1
  340.9 0.1 reshape.65
  341.0 8.5 %all-to-all-done.1 = f32[16,4,4,256]{3,2,1,0:T(4,128)S(1)} async-done(((f32[16,4,4,256]{3,2,1,0:T(4,128)}), f32[16,4,4,256]{3,2,1,0:T(4,128)S(1)}, u32[]{:S(2)}, u32[]{:S(2)}) %all-to-all-start.1) | async-done | bytes 262176 | tf_op jit(solution)/shard_map/all_to_all | solution.py:37
  349.5 0.6 gather_fusion.3
  350.0 0.7 copy_add_fusion
  (3 shorter events, 0.0 us)
Async XLA Ops:
  6.5 92.1 %copy-start = (s32[64,2]{0,1:T(2,128)S(1)}, s32[64,2]{0,1:T(2,128)}, u32[]{:S(2)}) copy-start(s32[64,2]{0,1:T(2,128)} %param.7) | copy-start | bytes 1540
  6.5 81.3 %all-gather.10.cloned.1.call-start = ((), (), s32[]{:S(2)}) async-start(), calls=%async_computation.4 | async-start | bytes 5570560 | tf_op jit(solution)/shard_map/all_gather | solution.py:14
  8.3 162.0 %all-gather.8.cloned.1.call-start = ((), (), s32[]{:S(2)}) async-start(), calls=%async_computation.3 | async-start | bytes 5570560 | tf_op jit(solution)/shard_map/all_gather | solution.py:57
  9.1 238.7 %all-gather.6.cloned.1.call-start = ((), (), s32[]{:S(2)}) async-start(), calls=%async_computation.2 | async-start | bytes 5570560 | tf_op jit(solution)/shard_map/all_gather | solution.py:58
  87.8 10.9 %copy-start.1 = (bf16[8,1024]{1,0:T(8,128)(2,1)S(1)}, bf16[8,1024]{1,0:T(8,128)(2,1)}, u32[]{:S(2)}) copy-start(bf16[8,1024]{1,0:T(8,128)(2,1)} %param.6) | copy-start | bytes 49156
  285.8 14.1 %copy-start.2 = (s32[128]{0:T(128)S(1)}, s32[128]{0:T(128)}, u32[]{:S(2)}) copy-start(s32[128]{0:T(128)} %param.9) | copy-start | bytes 1540
  286.7 54.1 %copy-start.3 = (s32[64]{0:T(128)S(1)}, s32[64]{0:T(128)}, u32[]{:S(2)}) copy-start(s32[64]{0:T(128)} %param.8) | copy-start | bytes 772
  287.6 44.5 %all-to-all-start = ((f32[32,4,1024]{2,1,0:T(4,128)}), f32[32,4,1024]{2,1,0:T(4,128)S(1)}, u32[]{:S(2)}, u32[]{:S(2)}) async-start(f32[32,4,1024]{2,1,0:T(4,128)} %reshape.27), calls=%async_computation | async-start | bytes 1048576 | tf_op jit(solution)/shard_map/all_to_all | solution.py:25
  333.9 15.5 %all-to-all-start.1 = ((f32[16,4,4,256]{3,2,1,0:T(4,128)}), f32[16,4,4,256]{3,2,1,0:T(4,128)S(1)}, u32[]{:S(2)}, u32[]{:S(2)}) async-start(f32[16,4,4,256]{3,2,1,0:T(4,128)} %broadcast_in_dim.42), calls=%async_computation.1 | async-start | bytes 524288 | tf_op jit(solution)/shard_map/all_to_all | solution.py:37
Sparse Core Ops, SparseCore 0:
  9.4 78.3 all-gather.9
  91.1 79.1 all-gather.7
  173.6 74.1 all-gather.5
